TPU v7x, 32 devices: a whole 2x2x4 slice. The times are simulated.
32 devices in a mesh: row: 8 (over z, y), col: 4 (over x, core).
Axes of the slice: x: 2, y: 2, z: 4, core: 2. Of those that a mesh axis runs over, the one named last changes fastest.
Arguments:
- noise: float32 [8192, 512], P(('row', 'col')), may hold values from -40 to 40
- data: float32 [8192, 512], P(('col', 'row')), may hold values from -6 to 6
Outputs:
- noise_target: float32 [8192, 512], P(('row', 'col'))
- data_target: float32 [8192, 512], P(('col', 'row'))
- f_potential: float32 [8192], P('row')
- g_potential: float32 [8192], P('col')
All inputs are finite; a program needn't handle non-finite values.
Results may differ from a plain program's by a relative error of at most 0.0003.
Values sent between devices are 32-bit elements; how exact they have to be, the bound alone decides.
A program may use at most 64 MiB of HBM per device.

v0:
```python
import jax
import jax.numpy as jnp
from jax import lax
from jax.sharding import PartitionSpec as P

ITERS = 2
EPSILON = 32.0


def row_stats(scores):
    peak = lax.pmax(jnp.max(scores, axis=1), "col")
    total = lax.psum(jnp.sum(jnp.exp(scores - peak[:, None]), axis=1), "col")
    return (peak, total)


def col_stats(scores):
    peak = lax.pmax(jnp.max(scores, axis=0), "row")
    total = lax.psum(jnp.sum(jnp.exp(scores - peak[None, :]), axis=0), "row")
    return (peak, total)


def shards(noise, data):
    x_full = lax.all_gather(noise, "col", axis=0, tiled=True)
    y_full = lax.all_gather(data, "row", axis=0, tiled=True)
    x_norm = jnp.sum(x_full * x_full, axis=1)
    y_norm = jnp.sum(y_full * y_full, axis=1)
    inner = jnp.dot(
        x_full, y_full.T, precision=lax.Precision.HIGHEST, preferred_element_type=jnp.float32
    )
    cost = x_norm[:, None] + y_norm[None, :] - 2.0 * inner
    g_now = jnp.zeros((cost.shape[1],), jnp.float32)
    f_now = jnp.zeros((cost.shape[0],), jnp.float32)
    col_scores = cost
    col_peak = g_now
    col_total = g_now
    for step in range(ITERS):
        row_scores = (g_now[None, :] - cost) / EPSILON
        peak, total = row_stats(row_scores)
        f_now = -EPSILON * (peak + jnp.log(total))
        col_scores = (f_now[:, None] - cost) / EPSILON
        col_peak, col_total = col_stats(col_scores)
        g_now = -EPSILON * (col_peak + jnp.log(col_total))
    col_weights = jnp.exp(col_scores - col_peak[None, :]) / col_total[None, :]
    data_part = jnp.dot(
        col_weights.T, x_full, precision=lax.Precision.HIGHEST, preferred_element_type=jnp.float32
    )
    data_target = lax.psum_scatter(data_part, "row", scatter_dimension=0, tiled=True)
    final_scores = (g_now[None, :] - cost) / EPSILON
    peak, total = row_stats(final_scores)
    weights = jnp.exp(final_scores - peak[:, None]) / total[:, None]
    noise_part = jnp.dot(
        weights, y_full, precision=lax.Precision.HIGHEST, preferred_element_type=jnp.float32
    )
    noise_target = lax.psum_scatter(noise_part, "col", scatter_dimension=0, tiled=True)
    return (noise_target, data_target, f_now, g_now)


def solution(mesh):
    placed = (P(("row", "col"), None), P(("col", "row"), None))
    return jax.shard_map(
        shards,
        mesh=mesh,
        in_specs=placed,
        out_specs=(P(("row", "col"), None), P(("col", "row"), None), P("row"), P("col")),
        check_vma=False,
    )
```

profile of v0, /device:TPU:0, one launch (start us, length us, event | category | flops | bytes accessed | tf_op | source)
XLA Modules:
  0.0 431.4 jit_solution(6373098548882051552)
XLA Ops:
  8.7 26.2 %all-gather.3.cloned.1.call-done = f32[1024,512]{1,0:T(8,128)} async-done(((f32[256,512]{1,0:T(8,128)}), f32[1024,512]{1,0:T(8,128)}) %all-gather.3.cloned.1.call-update) | async-done | bytes 2097168 | tf_op jit(solution)/shard_map/all_gather | solution.py:23
  36.7 73.1 %all-gather.5.cloned.1.call-done = f32[2048,512]{1,0:T(8,128)} async-done(((f32[256,512]{1,0:T(8,128)}), f32[2048,512]{1,0:T(8,128)}) %all-gather.5.cloned.1.call-update) | async-done | bytes 4194320 | tf_op jit(solution)/shard_map/all_gather | solution.py:24
  112.3 18.8 %fusion.4 = (f32[1024]{0:T(1024)S(1)}, f32[1024,2048]{1,0:T(8,128)}) fusion(f32[1024,512]{1,0:T(8,128)} %all-gather.3.cloned.1.call-done, f32[2048,512]{1,0:T(8,128)} %all-gather.5.cloned.1.call-done, f32[2048]{0:T(1024)S(1)} %multiply_reduce_fusion, f32[1024]{0:T(1024)S(1)} %multiply_reduce_fusion.1), kind=kOutput, calls=%fused_computation.15 | convolution fusion | flops 12897483776 | bytes 14696448 | tf_op jit(solution)/shard_map/dot_general | solution.py:27
  131.1 5.6 %pmax.35 = f32[1024]{0:T(1024)S(1)} all-reduce(f32[1024]{0:T(1024)S(1)} %get-tuple-element.4), channel_id=1, replica_groups=mesh['row'=8,'col'=4] {'col'}, use_global_device_ids=true, to_apply=%region_3.0 | all-reduce | flops 1024 | bytes 8192 | tf_op jit(solution)/shard_map/pmax | solution.py:11
  136.7 4.5 %exponential_reduce_fusion.2 = f32[1024]{0:T(1024)S(1)} fusion(f32[1024,2048]{1,0:T(8,128)} %get-tuple-element.5, f32[1024]{0:T(1024)S(1)} %pmax.35), kind=kLoop, calls=%fused_computation.12 | loop fusion | flops 8387584 | bytes 8396800 | tf_op jit(solution)/shard_map/reduce_sum | solution.py:12
  141.2 6.6 %psum.35 = f32[1024]{0:T(1024)S(1)} all-reduce(f32[1024]{0:T(1024)S(1)} %exponential_reduce_fusion.2), channel_id=1, replica_groups=mesh['row'=8,'col'=4] {'col'}, use_global_device_ids=true, to_apply=%region_5.0 | all-reduce | flops 1024 | bytes 8192 | tf_op jit(solution)/shard_map/psum | solution.py:12
  147.8 4.3 fusion.5
  152.1 19.2 %pmax.36 = f32[2048]{0:T(1024)S(1)} all-reduce(f32[2048]{0:T(1024)S(1)} %fusion.5), channel_id=1, replica_groups=mesh['row'=8,'col'=4] {'row'}, use_global_device_ids=true, to_apply=%region_7.0 | all-reduce | flops 2048 | bytes 16384 | tf_op jit(solution)/shard_map/pmax | solution.py:17
  171.4 4.5 %exponential_reduce_fusion.1 = f32[2048]{0:T(1024)S(1)} fusion(f32[1024,2048]{1,0:T(8,128)} %get-tuple-element.5, f32[2048]{0:T(1024)S(1)} %pmax.36, f32[1024]{0:T(1024)S(1)} %add_multiply_fusion.3), kind=kLoop, calls=%fused_computation.10 | loop fusion | flops 8386560 | bytes 8409088 | tf_op jit(solution)/shard_map/reduce_sum | solution.py:18
  175.9 17.7 %psum.36 = f32[2048]{0:T(1024)S(1)} all-reduce(f32[2048]{0:T(1024)S(1)} %exponential_reduce_fusion.1), channel_id=1, replica_groups=mesh['row'=8,'col'=4] {'row'}, use_global_device_ids=true, to_apply=%region_9.0 | all-reduce | flops 2048 | bytes 16384 | tf_op jit(solution)/shard_map/psum | solution.py:18
  197.9 5.7 %pmax.37 = f32[1024]{0:T(1024)S(1)} all-reduce(f32[1024]{0:T(1024)S(1)} %fusion.6), channel_id=1, replica_groups=mesh['row'=8,'col'=4] {'col'}, use_global_device_ids=true, to_apply=%region_11.0 | all-reduce | flops 1024 | bytes 8192 | tf_op jit(solution)/shard_map/pmax | solution.py:11
  203.6 4.5 %exponential_reduce_fusion = f32[1024]{0:T(1024)S(1)} fusion(f32[1024,2048]{1,0:T(8,128)} %get-tuple-element.5, f32[1024]{0:T(1024)S(1)} %pmax.37, f32[2048]{0:T(1024)S(1)} %add_multiply_fusion.1), kind=kLoop, calls=%fused_computation.8 | loop fusion | flops 8387584 | bytes 8404992 | tf_op jit(solution)/shard_map/reduce_sum | solution.py:12
  208.1 6.3 %psum.37 = f32[1024]{0:T(1024)S(1)} all-reduce(f32[1024]{0:T(1024)S(1)} %exponential_reduce_fusion), channel_id=1, replica_groups=mesh['row'=8,'col'=4] {'col'}, use_global_device_ids=true, to_apply=%region_13.0 | all-reduce | flops 1024 | bytes 8192 | tf_op jit(solution)/shard_map/psum | solution.py:12
  214.4 4.3 fusion.7
  218.6 19.1 %pmax.38 = f32[2048]{0:T(1024)S(1)} all-reduce(f32[2048]{0:T(1024)S(1)} %fusion.7), channel_id=1, replica_groups=mesh['row'=8,'col'=4] {'row'}, use_global_device_ids=true, to_apply=%region_15.0 | all-reduce | flops 2048 | bytes 16384 | tf_op jit(solution)/shard_map/pmax | solution.py:17
  237.8 4.5 %fusion.9 = f32[2048]{0:T(1024)S(1)} fusion(f32[1024,2048]{1,0:T(8,128)} %get-tuple-element.5, f32[2048]{0:T(1024)S(1)} %pmax.38, f32[1024]{0:T(1024)S(1)} %add_multiply_fusion.2), kind=kLoop, calls=%fused_computation.20 | loop fusion | flops 8386560 | bytes 8409088 | tf_op jit(solution)/shard_map/reduce_sum | solution.py:18
  242.3 17.7 %psum.38 = f32[2048]{0:T(1024)S(1)} all-reduce(f32[2048]{0:T(1024)S(1)} %fusion.9), channel_id=1, replica_groups=mesh['row'=8,'col'=4] {'row'}, use_global_device_ids=true, to_apply=%region_17.0 | all-reduce | flops 2048 | bytes 16384 | tf_op jit(solution)/shard_map/psum | solution.py:18
  264.3 5.7 %pmax.39 = f32[1024]{0:T(1024)S(1)} all-reduce(f32[1024]{0:T(1024)S(1)} %fusion.8), channel_id=1, replica_groups=mesh['row'=8,'col'=4] {'col'}, use_global_device_ids=true, to_apply=%region_19.0 | all-reduce | flops 1024 | bytes 8192 | tf_op jit(solution)/shard_map/pmax | solution.py:11
  270.0 4.5 %fusion.10 = f32[1024]{0:T(1024)S(1)} fusion(f32[1024,2048]{1,0:T(8,128)} %get-tuple-element.5, f32[1024]{0:T(1024)S(1)} %pmax.39, f32[2048]{0:T(1024)S(1)} %add_multiply_fusion), kind=kLoop, calls=%fused_computation.21 | loop fusion | flops 8387584 | bytes 8404992 | tf_op jit(solution)/shard_map/reduce_sum | solution.py:12
  274.4 6.5 %psum.39 = f32[1024]{0:T(1024)S(1)} all-reduce(f32[1024]{0:T(1024)S(1)} %fusion.10), channel_id=1, replica_groups=mesh['row'=8,'col'=4] {'col'}, use_global_device_ids=true, to_apply=%region_21.0 | all-reduce | flops 1024 | bytes 8192 | tf_op jit(solution)/shard_map/psum | solution.py:12
  281.0 22.4 %fusion.2 = f32[1024,512]{1,0:T(8,128)} fusion(f32[2048,512]{1,0:T(8,128)} %all-gather.5.cloned.1.call-done, f32[1024,2048]{1,0:T(8,128)} %get-tuple-element.5, f32[1024]{0:T(1024)S(1)} %psum.39, f32[1024]{0:T(1024)S(1)} %pmax.39, f32[2048]{0:T(1024)S(1)} %add_multiply_fusion), kind=kOutput, calls=%fused_computation.2 | convolution fusion | flops 12893290496 | bytes 14696448 | tf_op jit(solution)/shard_map/dot_general | solution.py:51
  303.7 18.5 %fusion = f32[2048,512]{1,0:T(8,128)} fusion(f32[1024,512]{1,0:T(8,128)S(1)} %copy-done, f32[1024,2048]{1,0:T(8,128)} %get-tuple-element.5, f32[2048]{0:T(1024)S(1)} %psum.38, f32[2048]{0:T(1024)S(1)} %pmax.38, f32[1024]{0:T(1024)S(1)} %add_multiply_fusion.2), kind=kOutput, calls=%fused_computation | convolution fusion | flops 12893290496 | bytes 14700544 | tf_op jit(solution)/shard_map/dot_general | solution.py:44
  322.3 10.3 %reduce-scatter.3.cloned.1.call-done = f32[256,512]{1,0:T(8,128)} async-done(((f32[1024,512]{1,0:T(8,128)}), f32[256,512]{1,0:T(8,128)}) %reduce-scatter.3.cloned.1.call-update) | async-done | bytes 524304 | tf_op jit(solution)/shard_map/reduce_scatter | solution.py:54
  332.5 92.4 %reduce-scatter.5.cloned.1.call-done = f32[256,512]{1,0:T(8,128)} async-done(((f32[2048,512]{1,0:T(8,128)}), f32[256,512]{1,0:T(8,128)}) %reduce-scatter.5.cloned.1.call-update) | async-done | bytes 524304 | tf_op jit(solution)/shard_map/reduce_scatter | solution.py:47
  (22 shorter events, 14.7 us)
Async XLA Ops:
  7.2 27.7 %all-gather.3.cloned.1.call-start = ((), (), s32[]{:S(2)}) async-start(), calls=%async_computation.2 | async-start | bytes 2621440 | tf_op jit(solution)/shard_map/all_gather | solution.py:23
  7.9 101.9 %all-gather.5.cloned.1.call-start = ((), (), s32[]{:S(2)}) async-start(), calls=%async_computation.3 | async-start | bytes 4718592 | tf_op jit(solution)/shard_map/all_gather | solution.py:24
  8.6 323.9 %reduce-scatter.3.cloned.1.call-start = ((), (), s32[]{:S(2)}) async-start(), calls=%async_computation.4 | async-start | bytes 2621440 | tf_op jit(solution)/shard_map/reduce_scatter | solution.py:54
  214.4 89.3 %copy-start.2 = (f32[1024]{0:T(1024)}, f32[1024]{0:T(1024)S(1)}, u32[]{:S(2)}) copy-start(f32[1024]{0:T(1024)S(1)} %add_multiply_fusion.2) | copy-start | bytes 12292
  260.0 21.0 %copy-start.1 = (f32[2048]{0:T(1024)}, f32[2048]{0:T(1024)S(1)}, u32[]{:S(2)}) copy-start(f32[2048]{0:T(1024)S(1)} %add_multiply_fusion) | copy-start | bytes 24580
  281.0 22.7 %copy-start = (f32[1024,512]{1,0:T(8,128)S(1)}, f32[1024,512]{1,0:T(8,128)}, u32[]{:S(2)}) copy-start(f32[1024,512]{1,0:T(8,128)} %all-gather.3.cloned.1.call-done) | copy-start | bytes 6291460
  303.4 121.5 %reduce-scatter.5.cloned.1.call-start = ((), (), s32[]{:S(2)}) async-start(), calls=%async_computation.5 | async-start | bytes 4718592 | tf_op jit(solution)/shard_map/reduce_scatter | solution.py:47
Sparse Core Ops, SparseCore 0:
  9.5 25.2 all-gather.2
  37.0 72.7 all-gather.4
  303.5 28.9 reduce-scatter.2
  336.6 88.2 reduce-scatter.4
where the time goes:
time: 432 us; the launch traced here: 431 us
  waiting for transfers between devices  203 us (47%)
  blocking collectives  110 us (25%)
  matrix products  59.7 us (14%)
  other arithmetic  43.9 us (10%)
  between operations  13.9 us (3%)
    reduce_scatter x1, waiting for transfers between devices, shards(): lax.psum_scatter(data_part, 'row', scatter_dimension=0, tiled=True)  92.4 us
    all_gather x1, waiting for transfers between devices, shards(): y_full = lax.all_gather(data, 'row', axis=0, tiled=True)  73.1 us
    pmax x2, blocking collectives, col_stats(): peak = lax.pmax(jnp.max(scores, axis=0), 'row')  38.4 us
    psum x2, blocking collectives, col_stats(): total = lax.psum(jnp.sum(jnp.exp(scores - peak[None, :]), axis=0), 'row')  35.4 us
    all_gather x1, waiting for transfers between devices, shards(): x_full = lax.all_gather(noise, 'col', axis=0, tiled=True)  26.2 us
    dot_general x1, matrix products, shards(): jnp.dot(weights, y_full, precision=lax.Precision.HIGHEST, preferred_eleme...  22.4 us
    psum x3, blocking collectives, row_stats(): total = lax.psum(jnp.sum(jnp.exp(scores - peak[:, None]), axis=1), 'col')  19.4 us
    dot_general x1, matrix products, shards(): jnp.dot(x_full, y_full.T, precision=lax.Precision.HIGHEST, preferred_elem...  18.8 us
  transfers between devices with their start and end apart: 4, of which 4 were waited for; matrix products, arithmetic and copies ran while one was open for 5% of the time, Pallas kernels for 0%

commit v1 on v0

--- a/solution.py
+++ b/solution.py
@@ -15,7 +15,7 @@
 
 def col_stats(scores):
     peak = lax.pmax(jnp.max(scores, axis=0), "row")
-    total = lax.psum(jnp.sum(jnp.exp(scores - peak[None, :]), axis=0), "row")
+    total = jnp.sum(lax.all_gather(jnp.sum(jnp.exp(scores - peak[None, :]), axis=0), "row"), axis=0)
     return (peak, total)
 
 

time: 432 us -> 456 us (1.056)
  blocking collectives: 110 us -> 134 us
    all_gather x0 -> x2, blocking collectives: none -> 61.3 us  [col_stats(): lax.all_gather(jnp.sum(jnp.exp(scores - peak[None, :]), axis=0), 'row')]
    psum x2 -> x0, blocking collectives: 35.4 us -> none  [col_stats(): total = lax.psum(jnp.sum(jnp.exp(scores - peak[None, :]), axis=0), 'row')]
  transfers between devices with their start and end apart: 4 -> 4, of which waited for: 4 -> 4; matrix products, arithmetic and copies ran while one was open for 5% -> 4% of each run, Pallas kernels for 0% -> 0%
where the time goes in v1:
time: 456 us
  waiting for transfers between devices  203 us (45%)
  blocking collectives  134 us (29%)
  matrix products  59.7 us (13%)
  other arithmetic  44 us (10%)
  between operations  13.9 us (3%)
    reduce_scatter x1, waiting for transfers between devices, shards(): lax.psum_scatter(data_part, 'row', scatter_dimension=0, tiled=True)  92.4 us
    all_gather x1, waiting for transfers between devices, shards(): y_full = lax.all_gather(data, 'row', axis=0, tiled=True)  73.1 us
    all_gather x2, blocking collectives, col_stats(): lax.all_gather(jnp.sum(jnp.exp(scores - peak[None, :]), axis=0), 'row')  61.3 us
    pmax x2, blocking collectives, col_stats(): peak = lax.pmax(jnp.max(scores, axis=0), 'row')  36.9 us
    all_gather x1, waiting for transfers between devices, shards(): x_full = lax.all_gather(noise, 'col', axis=0, tiled=True)  26.2 us
    dot_general x1, matrix products, shards(): jnp.dot(weights, y_full, precision=lax.Precision.HIGHEST, preferred_eleme...  22.4 us
    psum x3, blocking collectives, row_stats(): total = lax.psum(jnp.sum(jnp.exp(scores - peak[:, None]), axis=1), 'col')  19.3 us
    dot_general x1, matrix products, shards(): jnp.dot(x_full, y_full.T, precision=lax.Precision.HIGHEST, preferred_elem...  18.8 us
  transfers between devices with their start and end apart: 4, of which 4 were waited for; matrix products, arithmetic and copies ran while one was open for 4% of the time, Pallas kernels for 0%

profile of v1, /device:TPU:0, one launch (start us, length us, event | category | flops | bytes accessed | tf_op | source)
XLA Modules:
  0.0 455.9 jit_solution(15734581166364021045)
XLA Ops:
  8.7 26.2 %all-gather.5.cloned.1.call-done = f32[1024,512]{1,0:T(8,128)} async-done(((f32[256,512]{1,0:T(8,128)}), f32[1024,512]{1,0:T(8,128)}) %all-gather.5.cloned.1.call-update) | async-done | bytes 2097168 | tf_op jit(solution)/shard_map/all_gather | solution.py:23
  36.7 73.1 %all-gather.7.cloned.1.call-done = f32[2048,512]{1,0:T(8,128)} async-done(((f32[256,512]{1,0:T(8,128)}), f32[2048,512]{1,0:T(8,128)}) %all-gather.7.cloned.1.call-update) | async-done | bytes 4194320 | tf_op jit(solution)/shard_map/all_gather | solution.py:24
  112.3 18.8 %fusion.4 = (f32[1024]{0:T(1024)S(1)}, f32[1024,2048]{1,0:T(8,128)}) fusion(f32[1024,512]{1,0:T(8,128)} %all-gather.5.cloned.1.call-done, f32[2048,512]{1,0:T(8,128)} %all-gather.7.cloned.1.call-done, f32[2048]{0:T(1024)S(1)} %multiply_reduce_fusion, f32[1024]{0:T(1024)S(1)} %multiply_reduce_fusion.1), kind=kOutput, calls=%fused_computation.15 | convolution fusion | flops 12897483776 | bytes 14696448 | tf_op jit(solution)/shard_map/dot_general | solution.py:27
  131.1 5.6 %pmax.35 = f32[1024]{0:T(1024)S(1)} all-reduce(f32[1024]{0:T(1024)S(1)} %get-tuple-element.4), channel_id=1, replica_groups=mesh['row'=8,'col'=4] {'col'}, use_global_device_ids=true, to_apply=%region_3.0 | all-reduce | flops 1024 | bytes 8192 | tf_op jit(solution)/shard_map/pmax | solution.py:11
  136.7 4.5 exponential_reduce_fusion.2
  141.2 6.6 %psum.21 = f32[1024]{0:T(1024)S(1)} all-reduce(f32[1024]{0:T(1024)S(1)} %exponential_reduce_fusion.2), channel_id=1, replica_groups=mesh['row'=8,'col'=4] {'col'}, use_global_device_ids=true, to_apply=%region_5.0 | all-reduce | flops 1024 | bytes 8192 | tf_op jit(solution)/shard_map/psum | solution.py:12
  147.8 4.3 fusion.5
  152.1 19.2 %pmax.36 = f32[2048]{0:T(1024)S(1)} all-reduce(f32[2048]{0:T(1024)S(1)} %fusion.5), channel_id=1, replica_groups=mesh['row'=8,'col'=4] {'row'}, use_global_device_ids=true, to_apply=%region_7.0 | all-reduce | flops 2048 | bytes 16384 | tf_op jit(solution)/shard_map/pmax | solution.py:17
  171.4 4.5 exponential_reduce_fusion.1
  175.9 30.7 %all-gather = f32[16384]{0:T(1024)S(1)} all-gather(f32[2048]{0:T(1024)S(1)} %exponential_reduce_fusion.1), channel_id=2, replica_groups=mesh['row'=8,'col'=4] {'row'}, dimensions={0}, use_global_device_ids=true | all-gather | bytes 73728 | tf_op jit(solution)/shard_map/all_gather | solution.py:18
  210.9 5.7 %pmax.37 = f32[1024]{0:T(1024)S(1)} all-reduce(f32[1024]{0:T(1024)S(1)} %fusion.6), channel_id=1, replica_groups=mesh['row'=8,'col'=4] {'col'}, use_global_device_ids=true, to_apply=%region_11.0 | all-reduce | flops 1024 | bytes 8192 | tf_op jit(solution)/shard_map/pmax | solution.py:11
  216.6 4.5 exponential_reduce_fusion
  221.1 6.2 %psum.22 = f32[1024]{0:T(1024)S(1)} all-reduce(f32[1024]{0:T(1024)S(1)} %exponential_reduce_fusion), channel_id=1, replica_groups=mesh['row'=8,'col'=4] {'col'}, use_global_device_ids=true, to_apply=%region_13.0 | all-reduce | flops 1024 | bytes 8192 | tf_op jit(solution)/shard_map/psum | solution.py:12
  227.3 4.3 fusion.7
  231.6 17.6 %pmax.38 = f32[2048]{0:T(1024)S(1)} all-reduce(f32[2048]{0:T(1024)S(1)} %fusion.7), channel_id=1, replica_groups=mesh['row'=8,'col'=4] {'row'}, use_global_device_ids=true, to_apply=%region_15.0 | all-reduce | flops 2048 | bytes 16384 | tf_op jit(solution)/shard_map/pmax | solution.py:17
  249.2 4.5 fusion.9
  253.7 30.5 %all-gather.1 = f32[16384]{0:T(1024)S(1)} all-gather(f32[2048]{0:T(1024)S(1)} %fusion.9), channel_id=3, replica_groups=mesh['row'=8,'col'=4] {'row'}, dimensions={0}, use_global_device_ids=true | all-gather | bytes 73728 | tf_op jit(solution)/shard_map/all_gather | solution.py:18
  288.6 5.7 %pmax.39 = f32[1024]{0:T(1024)S(1)} all-reduce(f32[1024]{0:T(1024)S(1)} %fusion.8), channel_id=1, replica_groups=mesh['row'=8,'col'=4] {'col'}, use_global_device_ids=true, to_apply=%region_19.0 | all-reduce | flops 1024 | bytes 8192 | tf_op jit(solution)/shard_map/pmax | solution.py:11
  294.3 4.5 fusion.10
  298.8 6.5 %psum.23 = f32[1024]{0:T(1024)S(1)} all-reduce(f32[1024]{0:T(1024)S(1)} %fusion.10), channel_id=1, replica_groups=mesh['row'=8,'col'=4] {'col'}, use_global_device_ids=true, to_apply=%region_21.0 | all-reduce | flops 1024 | bytes 8192 | tf_op jit(solution)/shard_map/psum | solution.py:12
  305.3 22.4 %fusion.2 = f32[1024,512]{1,0:T(8,128)} fusion(f32[2048,512]{1,0:T(8,128)} %all-gather.7.cloned.1.call-done, f32[1024,2048]{1,0:T(8,128)} %get-tuple-element.5, f32[1024]{0:T(1024)S(1)} %psum.23, f32[1024]{0:T(1024)S(1)} %pmax.39, f32[2048]{0:T(1024)S(1)} %add_multiply_fusion), kind=kOutput, calls=%fused_computation.2 | convolution fusion | flops 12893290496 | bytes 14696448 | tf_op jit(solution)/shard_map/dot_general | solution.py:51
  328.0 18.5 %fusion = f32[2048,512]{1,0:T(8,128)} fusion(f32[1024,512]{1,0:T(8,128)S(1)} %copy-done, f32[1024,2048]{1,0:T(8,128)} %get-tuple-element.5, f32[2048]{0:T(1024)S(1)} %reduce_sum.88, f32[2048]{0:T(1024)S(1)} %pmax.38, f32[1024]{0:T(1024)S(1)} %add_multiply_fusion.2), kind=kOutput, calls=%fused_computation | convolution fusion | flops 12893290496 | bytes 14700544 | tf_op jit(solution)/shard_map/dot_general | solution.py:44
  346.6 10.4 %reduce-scatter.3.cloned.1.call-done = f32[256,512]{1,0:T(8,128)} async-done(((f32[1024,512]{1,0:T(8,128)}), f32[256,512]{1,0:T(8,128)}) %reduce-scatter.3.cloned.1.call-update) | async-done | bytes 524304 | tf_op jit(solution)/shard_map/reduce_scatter | solution.py:54
  356.9 92.4 %reduce-scatter.5.cloned.1.call-done = f32[256,512]{1,0:T(8,128)} async-done(((f32[2048,512]{1,0:T(8,128)}), f32[256,512]{1,0:T(8,128)}) %reduce-scatter.5.cloned.1.call-update) | async-done | bytes 524304 | tf_op jit(solution)/shard_map/reduce_scatter | solution.py:47
  (26 shorter events, 14.8 us)
Async XLA Ops:
  7.2 27.7 %all-gather.5.cloned.1.call-start = ((), (), s32[]{:S(2)}) async-start(), calls=%async_computation.2 | async-start | bytes 2621440 | tf_op jit(solution)/shard_map/all_gather | solution.py:23
  7.9 101.9 %all-gather.7.cloned.1.call-start = ((), (), s32[]{:S(2)}) async-start(), calls=%async_computation.3 | async-start | bytes 4718592 | tf_op jit(solution)/shard_map/all_gather | solution.py:24
  8.6 348.3 %reduce-scatter.3.cloned.1.call-start = ((), (), s32[]{:S(2)}) async-start(), calls=%async_computation.4 | async-start | bytes 2621440 | tf_op jit(solution)/shard_map/reduce_scatter | solution.py:54
  227.3 100.7 %copy-start.2 = (f32[1024]{0:T(1024)}, f32[1024]{0:T(1024)S(1)}, u32[]{:S(2)}) copy-start(f32[1024]{0:T(1024)S(1)} %add_multiply_fusion.2) | copy-start | bytes 12292
  284.3 20.9 %copy-start.1 = (f32[2048]{0:T(1024)}, f32[2048]{0:T(1024)S(1)}, u32[]{:S(2)}) copy-start(f32[2048]{0:T(1024)S(1)} %add_multiply_fusion) | copy-start | bytes 24580
  305.3 22.7 %copy-start = (f32[1024,512]{1,0:T(8,128)S(1)}, f32[1024,512]{1,0:T(8,128)}, u32[]{:S(2)}) copy-start(f32[1024,512]{1,0:T(8,128)} %all-gather.5.cloned.1.call-done) | copy-start | bytes 6291460
  327.7 121.6 %reduce-scatter.5.cloned.1.call-start = ((), (), s32[]{:S(2)}) async-start(), calls=%async_computation.5 | async-start | bytes 4718592 | tf_op jit(solution)/shard_map/reduce_scatter | solution.py:47
Sparse Core Ops, SparseCore 0:
  9.5 25.2 all-gather.4
  37.0 72.7 all-gather.6
  327.9 29.0 reduce-scatter.2
  361.0 88.2 reduce-scatter.4
